TPU v7x, 32 devices: a whole 2x2x4 slice. The times are simulated.
32 devices in a mesh: tok: 4 (over y, x), col: 8 (over z, core).
Axes of the slice: x: 2, y: 2, z: 4, core: 2. Of those that a mesh axis runs over, the one named last changes fastest.
Arguments:
- row_bank: bfloat16 [16384, 8192], P(None, 'col'), may hold values from -50 to 50
- token_ids: int32 [6144], P('tok'), may hold values from 0 to 16383
- sign_flips: int32 [8192], P('col'), may hold values from -1 to 1, as said below
- damping: float32 [1], replicated, may hold values from 0.1 to 1
Outputs:
- hessian: float32 [8192, 8192], P('tok', 'col')
Inputs may be any that keep to these rules, and one draw needn't show every extreme that they name: `sign_flips`: each entry is -1 or 1.
All inputs are finite; a program needn't handle non-finite values.
Results may differ from a plain program's by a relative error of at most 0.0003.
The roundings to bfloat16 on the way count: a program that leaves them out, or rounds other values in their place, can miss the bound.
Values may be sent and summed in bfloat16 or wider, within the bound.
A program may use at most 192 MiB of HBM per device.

v0:
```python
import functools
import math

import jax
import jax.numpy as jnp
import numpy as np
from jax import lax
from jax.experimental import pallas as pl
from jax.experimental.pallas import tpu as pltpu
from jax.sharding import PartitionSpec as P

D = 8192
BLOCK = 32
LANES = 512
MESH = pl.DeviceIdType.MESH


def hadamard(order):
    index_range = jnp.arange(order, dtype=jnp.int32)
    anded = jnp.bitwise_and(index_range[:, None], index_range[None, :])
    parity = jnp.zeros((order, order), jnp.int32)
    for bit_place in range(int(order).bit_length()):
        parity = parity + jnp.bitwise_and(jnp.right_shift(anded, bit_place), 1)
    return (1 - 2 * jnp.bitwise_and(parity, 1)).astype(jnp.bfloat16)


def sylvester(order):
    table = np.ones((1, 1))
    while table.shape[0] < order:
        table = np.block([[table, table], [table, -table]])
    return table


def fused_kernel(
    planes, chunks, rows, piece, scale,
    half_ref, table_ref,
    gram_ref, gram_in_ref, square_ref, full_ref,
    xbuf, tmp, rot, rxr, rxq, acc, squares,
    part_send, part_recv, z_send, z_recv, r_send, r_recv, q_send, q_recv,
    s_send, s_recv, g_send, g_recv, load_sem, out_sem,
):
    tok = lax.axis_index("tok")
    col = lax.axis_index("col")
    plane, core = col // 2, col % 2
    mate = plane * 2 + (1 - core)
    ypos, xpos = tok // 2, tok % 2
    peers = {1: ypos * 2 + (1 - xpos), 2: (1 - ypos) * 2 + xpos, 3: 3 - tok}
    wide = 2 * piece

    barrier = pltpu.get_barrier_semaphore()
    greet = [(tok, mate)]
    for m in (1, 2, 3):
        greet.append((peers[m], col))
        greet.append((peers[m], mate))
    for m in range(1, planes):
        greet.append((tok, ((plane + m) % planes) * 2 + core))
    for device in greet:
        pl.semaphore_signal(barrier, inc=1, device_id=device, device_id_type=MESH)
    pl.semaphore_wait(barrier, len(greet))

    def part_copy(k):
        return pltpu.make_async_remote_copy(
            src_ref=half_ref.at[1 - core, k], dst_ref=full_ref.at[k, col],
            send_sem=part_send.at[k], recv_sem=part_recv.at[k],
            device_id=(tok, mate), device_id_type=MESH)

    def part_arrival(k):
        return pltpu.make_async_remote_copy(
            src_ref=half_ref.at[1 - core, k], dst_ref=full_ref.at[k, mate],
            send_sem=part_send.at[k], recv_sem=part_recv.at[k],
            device_id=(tok, mate), device_id_type=MESH)

    def z_copy(k, j, way, own=False):
        source = half_ref.at[core, k] if own else full_ref.at[k, j]
        return pltpu.make_async_remote_copy(
            src_ref=source, dst_ref=full_ref.at[k, j],
            send_sem=z_send.at[k, j, way], recv_sem=z_recv.at[k, j],
            device_id=(tok, col + 2 - 4 * way), device_id_type=MESH)

    can = {0: plane < planes - 1, 1: plane > 0}

    def own_sends(k):
        for way in (0, 1):
            @pl.when(can[way])
            def _():
                z_copy(k, col, way, own=True).start()
        part_arrival(k).wait_recv()
        for way in (0, 1):
            @pl.when(can[way])
            def _():
                z_copy(k, mate, way).start()

    def row_copy(k, m):
        return pltpu.make_async_remote_copy(
            src_ref=rot.at[k, pl.ds(peers[m] * wide, wide)],
            dst_ref=rxr.at[k, :, pl.ds(m * rows, rows)],
            send_sem=r_send.at[k, m], recv_sem=r_recv.at[k, m],
            device_id=(peers[m], col), device_id_type=MESH)

    def col_copy(k, m):
        return pltpu.make_async_remote_copy(
            src_ref=rot.at[k, pl.ds(plane * wide, wide)],
            dst_ref=rxq.at[k, :, pl.ds(m * rows, rows)],
            send_sem=q_send.at[k, m], recv_sem=q_recv.at[k, m],
            device_id=(peers[m], col), device_id_type=MESH)

    def relay_copy(k):
        odd = k % 2
        target = peers[2] * (1 - odd) + peers[1] * odd
        start = pl.multiple_of((1 + odd) * rows, rows)
        return pltpu.make_async_remote_copy(
            src_ref=rxq.at[k, :, pl.ds(start, rows)],
            dst_ref=rxq.at[k, :, pl.ds(3 * rows, rows)],
            send_sem=q_send.at[k, 3], recv_sem=q_recv.at[k, 3],
            device_id=(target, col), device_id_type=MESH)

    def z_stage(k, distance):
        for way, origin in ((0, plane - distance), (1, plane + distance)):
            @pl.when((origin >= 0) & (origin < planes))
            def _():
                for side in (0, 1):
                    j = origin * 2 + (core if side == 0 else 1 - core)
                    z_copy(k, j, way).wait_recv()

                    @pl.when(can[way])
                    def _():
                        z_copy(k, j, way).start()

    def load_chunk(k):
        copies = [pltpu.make_async_copy(half_ref.at[core, k], xbuf.at[col], load_sem.at[0])]
        copies.append(pltpu.make_async_copy(full_ref.at[k, mate], xbuf.at[mate], load_sem.at[1]))
        for m in range(1, planes):
            other = ((plane + m) % planes) * 2
            copies.append(pltpu.make_async_copy(
                full_ref.at[k, pl.ds(other, 2)], xbuf.at[pl.ds(other, 2)], load_sem.at[1 + m]))
        for copy in copies:
            copy.start()
        for copy in copies:
            copy.wait()

    groups = 2 * planes * piece

    def rotate(k):
        def product(j, carry):
            block = xbuf[j].reshape(piece * rows, LANES)
            out = jnp.dot(block, table_ref[...], preferred_element_type=jnp.float32)
            tmp[pl.ds(j * piece, piece)] = out.reshape(piece, rows, LANES)
            return carry

        lax.fori_loop(0, 2 * planes, product, 0)

        def butterfly(index, carry):
            r = pl.multiple_of((index // (LANES // 128)) * 16, 16)
            lane = pl.multiple_of((index % (LANES // 128)) * 128, 128)
            values = [tmp[g, pl.ds(r, 16), pl.ds(lane, 128)] for g in range(groups)]
            step = 1
            while step < groups:
                values = [
                    values[g] + values[g + step] if g & step == 0 else values[g - step] - values[g]
                    for g in range(groups)
                ]
                step *= 2
            total = squares[0]
            for g in range(groups):
                rounded = (values[g] * scale).astype(jnp.bfloat16)
                rot[k, g, pl.ds(r, 16), pl.ds(lane, 128)] = rounded
                exact = rounded.astype(jnp.float32)
                total = total + exact * exact
            squares[0] = total
            return carry

        lax.fori_loop(0, (rows // 16) * (LANES // 128), butterfly, 0)
        for f in range(wide):
            rxr[k, f, pl.ds(0, rows)] = rot[k, tok * wide + f]
            rxq[k, f, pl.ds(0, rows)] = rot[k, plane * wide + f]
        for m in (1, 2):
            col_copy(k, m).start()
        for m in (1, 2, 3):
            row_copy(k, m).start()

    def relay(k):
        odd = k % 2

        @pl.when(odd == 0)
        def _():
            col_copy(k, 1).wait_recv()

        @pl.when(odd == 1)
        def _():
            col_copy(k, 2).wait_recv()

        relay_copy(k).start()

    def arrivals(k):
        odd = k % 2

        @pl.when(odd == 0)
        def _():
            col_copy(k, 2).wait_recv()

        @pl.when(odd == 1)
        def _():
            col_copy(k, 1).wait_recv()

        for m in (1, 2, 3):
            row_copy(k, m).wait_recv()
        relay_copy(k).wait_recv()

    def row_block(k, f):
        left = rxr[k, f].T
        start = pl.multiple_of(f * LANES, LANES)
        for n in range(wide):
            out = jnp.dot(left, rxq[k, n], preferred_element_type=jnp.float32)
            acc[n // piece, pl.ds(start, LANES), pl.ds((n % piece) * LANES, LANES)] += out

    def gram(k):
        def body(f, carry):
            row_block(k, f)
            return carry

        lax.fori_loop(0, wide, body, 0)

    def gram_out(f):
        span = pl.ds(pl.multiple_of(f * LANES, LANES), LANES)
        return pltpu.make_async_remote_copy(
            src_ref=acc.at[1 - core, span], dst_ref=gram_in_ref.at[span],
            send_sem=g_send.at[f], recv_sem=g_recv.at[f],
            device_id=(tok, mate), device_id_type=MESH)

    def gram_keep(f):
        span = pl.ds(pl.multiple_of(f * LANES, LANES), LANES)
        return pltpu.make_async_copy(acc.at[core, span], gram_ref.at[span], out_sem.at[f])

    def square_copy(m):
        target = (tok, mate) if m == 4 else (peers[m % 4], col if m < 4 else mate)
        return pltpu.make_async_remote_copy(
            src_ref=squares.at[0], dst_ref=squares.at[m],
            send_sem=s_send.at[m], recv_sem=s_recv.at[m],
            device_id=target, device_id_type=MESH)

    def send_part(k, carry):
        part_copy(k).start()
        return carry

    lax.fori_loop(0, chunks, send_part, 0)
    own_sends(0)
    squares[0] = jnp.zeros((16, 128), jnp.float32)

    def clear(index, carry):
        start = pl.multiple_of((index % (acc.shape[1] // 64)) * 64, 64)
        acc[index // (acc.shape[1] // 64), pl.ds(start, 64)] = jnp.zeros((64, acc.shape[2]), jnp.float32)
        return carry

    lax.fori_loop(0, acc.shape[0] * (acc.shape[1] // 64), clear, 0)
    for distance in range(1, planes - 1):
        z_stage(0, distance)
    if chunks > 1:
        own_sends(1)

    def step(k, carry):
        z_stage(k, planes - 1)
        if planes > 2:
            @pl.when(k + 1 < chunks)
            def _():
                z_stage(k + 1, 1)

        @pl.when(k + 2 < chunks)
        def _():
            own_sends(k + 2)

        @pl.when(k > 0)
        def _():
            relay(k - 1)

        load_chunk(k)
        rotate(k)

        @pl.when(k + 1 < chunks)
        def _():
            for distance in range(2, planes - 1):
                z_stage(k + 1, distance)

        @pl.when(k > 1)
        def _():
            arrivals(k - 2)
            gram(k - 2)

        return carry

    lax.fori_loop(0, chunks, step, 0)
    for m in range(1, 8):
        square_copy(m).start()
    last = chunks - 1
    if chunks > 1:
        arrivals(last - 1)
        gram(last - 1)
    relay(last)
    arrivals(last)

    def final(f, carry):
        row_block(last, f)

        @pl.when(f > 0)
        def _():
            gram_out(f - 1).start()
            gram_keep(f - 1).start()

        return carry

    lax.fori_loop(0, wide, final, 0)
    for m in range(1, 8):
        square_copy(m).wait()
    sums = squares[0]
    for m in range(1, 8):
        sums = sums + squares[m]
    square_ref[...] = sums
    gram_out(wide - 1).start()
    gram_keep(wide - 1).start()

    def drain(k, carry):
        part_copy(k).wait_send()
        for j in range(2 * planes):
            @pl.when(can[0] & (j // 2 <= plane))
            def _():
                z_copy(k, j, 0).wait_send()

            @pl.when(can[1] & (j // 2 >= plane))
            def _():
                z_copy(k, j, 1).wait_send()
        for m in (1, 2):
            col_copy(k, m).wait_send()
        relay_copy(k).wait_send()
        for m in (1, 2, 3):
            row_copy(k, m).wait_send()
        return carry

    lax.fori_loop(0, chunks, drain, 0)

    def finish(f, carry):
        gram_out(f).wait()
        gram_keep(f).wait()
        return carry

    lax.fori_loop(0, wide, finish, 0)


def fits(row_bank, token_ids):
    col_width, tok_rows = row_bank.shape[1], token_ids.shape[0]
    col_count, tok_count = lax.axis_size("col"), lax.axis_size("tok")
    return (
        col_width % LANES == 0
        and tok_count == 4
        and col_count % 2 == 0
        and D // tok_count == 2 * col_width
        and tok_rows % 256 == 0
        and tok_rows * D * 6 + (D // tok_count) ** 2 * 4 <= 96 * 2**20
    )


def fused(row_bank, token_ids, sign_flips, damping):
    col_width = row_bank.shape[1]
    col_count = lax.axis_size("col")
    tok_count = lax.axis_size("tok")
    tok_rows = token_ids.shape[0]
    planes = col_count // 2
    own_rows = tok_rows // 2
    rows = 64
    chunks = own_rows // rows
    piece = col_width // LANES
    wide = 2 * piece
    groups = D // LANES
    spread = LANES // BLOCK
    inner = jnp.asarray(np.kron(np.eye(spread), sylvester(BLOCK)), jnp.bfloat16)
    outer = jnp.asarray(np.kron(sylvester(spread), np.eye(BLOCK)), jnp.bfloat16)
    signs = sign_flips.astype(jnp.bfloat16)[:, None]
    picked = jnp.take(row_bank, token_ids, axis=0)
    parts = []
    for g in range(piece):
        part = picked[:, g * LANES : (g + 1) * LANES]
        table = inner * signs[g * LANES : (g + 1) * LANES]
        part = jnp.dot(part, table, preferred_element_type=jnp.float32).astype(jnp.bfloat16)
        parts.append(part.reshape(2, chunks, rows, LANES))
    half = jnp.stack(parts, axis=2)
    any_space = pl.BlockSpec(memory_space=pl.ANY)
    vmem = pl.BlockSpec(memory_space=pltpu.VMEM)
    dma = pltpu.SemaphoreType.DMA
    height = D // tok_count
    gram, gram_in, squares, _ = pl.pallas_call(
        functools.partial(fused_kernel, planes, chunks, rows, piece, 1.0 / math.sqrt(D)),
        out_shape=(
            jax.ShapeDtypeStruct((height, col_width), jnp.float32),
            jax.ShapeDtypeStruct((height, col_width), jnp.float32),
            jax.ShapeDtypeStruct((16, 128), jnp.float32),
            jax.ShapeDtypeStruct((chunks, col_count, piece, rows, LANES), jnp.bfloat16),
        ),
        in_specs=[any_space, vmem],
        out_specs=(any_space, any_space, vmem, any_space),
        scratch_shapes=[
            pltpu.VMEM((col_count, piece, rows, LANES), jnp.bfloat16),
            pltpu.VMEM((groups, rows, LANES), jnp.float32),
            pltpu.VMEM((chunks, groups, rows, LANES), jnp.bfloat16),
            pltpu.VMEM((chunks, wide, 4 * rows, LANES), jnp.bfloat16),
            pltpu.VMEM((chunks, wide, 4 * rows, LANES), jnp.bfloat16),
            pltpu.VMEM((2, height, col_width), jnp.float32),
            pltpu.VMEM((8, 16, 128), jnp.float32),
            dma((chunks,)), dma((chunks,)),
            dma((chunks, col_count, 2)), dma((chunks, col_count)),
            dma((chunks, 4)), dma((chunks, 4)),
            dma((chunks, 4)), dma((chunks, 4)),
            dma((8,)), dma((8,)),
            dma((wide,)), dma((wide,)),
            dma((planes + 1,)), dma((wide,)),
        ],
        compiler_params=pltpu.CompilerParams(
            collective_id=0, has_side_effects=True, vmem_limit_bytes=67043328
        ),
    )(half, outer)
    tokens_all = tok_rows * tok_count
    mean_diag = jnp.sum(squares) / tokens_all / D
    gram_block = (gram + gram_in) / tokens_all
    return damped(gram_block, damping, mean_diag)


def damped(gram_block, damping, mean_diag):
    block_rows, col_width = gram_block.shape
    row_index = lax.axis_index("tok") * block_rows + lax.broadcasted_iota(
        jnp.int32, gram_block.shape, 0
    )
    col_index = lax.axis_index("col") * col_width + lax.broadcasted_iota(
        jnp.int32, gram_block.shape, 1
    )
    on_diag = (row_index == col_index).astype(jnp.float32)
    return gram_block + damping[0] * mean_diag * on_diag


def plain(row_bank, token_ids, sign_flips, damping):
    col_width = row_bank.shape[1]
    col_count = lax.axis_size("col")
    tok_count = lax.axis_size("tok")
    tok_rows = token_ids.shape[0]
    groups = D // BLOCK
    scale = 1.0 / math.sqrt(D)
    inner_table = hadamard(BLOCK)
    outer_table = hadamard(groups)
    col_start = lax.axis_index("col") * col_width
    picked = jnp.take(row_bank, token_ids, axis=0) * sign_flips.astype(jnp.bfloat16)[None, :]
    shaped = picked.reshape(picked.shape[0], -1, BLOCK)
    turned = jnp.einsum("rab,bc->rac", shaped, inner_table, preferred_element_type=jnp.float32)
    half_turned = turned.astype(jnp.bfloat16).reshape(picked.shape)
    grouped = half_turned.reshape(col_count, tok_rows // col_count, col_width)
    block = lax.all_to_all(grouped, "col", split_axis=0, concat_axis=2, tiled=True)[0]
    shaped = block.reshape(block.shape[0], groups, BLOCK)
    turned = (
        jnp.einsum("rab,ac->rcb", shaped, outer_table, preferred_element_type=jnp.float32) * scale
    )
    finished = turned.astype(jnp.bfloat16).reshape(block.shape)[None]
    squares = jnp.sum(jnp.square(finished.astype(jnp.float32)))
    tokens_all = tok_rows * tok_count
    square_sum = lax.psum(squares, ("tok", "col"))
    mean_diag = square_sum / tokens_all / D
    flat = lax.all_gather(finished, "col", axis=1, tiled=True).reshape(-1, D)
    own_cols = lax.dynamic_slice_in_dim(flat, col_start, col_width, 1)
    partial_sum = lax.dot_general(
        flat, own_cols, (((0,), (0,)), ((), ())), preferred_element_type=jnp.float32
    )
    gram_block = lax.psum_scatter(partial_sum, "tok", scatter_dimension=0, tiled=True) / tokens_all
    return damped(gram_block, damping, mean_diag)


def shards(row_bank, token_ids, sign_flips, damping):
    run = fused if fits(row_bank, token_ids) else plain
    return run(row_bank, token_ids, sign_flips, damping)


def solution(mesh):
    in_specs = (P(None, "col"), P("tok"), P("col"), P())
    out_specs = P("tok", "col")
    return jax.shard_map(shards, mesh=mesh, in_specs=in_specs, out_specs=out_specs, check_vma=False)
```

profile of v0, /device:TPU:3, one launch (start us, length us, event | category | flops | bytes accessed | tf_op | source)
XLA Modules:
  0.0 322.8 jit_solution(9135410047877539953)
XLA Ops:
  0.0 0.7 compare_select_fusion
  0.7 0.0 copy-start
  0.7 11.4 %gather_fusion = bf16[1536,1024]{1,0:T(8,128)(2,1)S(1)} fusion(bf16[16384,1024]{1,0:T(8,128)(2,1)} %param.6, s32[2048]{0:T(1024)S(1)} %pad_clamp_fusion), kind=kCustom, calls=%fused_computation | custom fusion | bytes 6297600 | tf_op jit(solution)/shard_map/jit(_take)/gather | solution.py:376
  12.1 0.0 copy-done
  12.2 0.0 copy-start.1
  12.2 0.0 copy-start.2
  12.2 0.9 broadcast_select_fusion
  13.1 0.0 copy-done.1
  13.2 0.1 copy-done.2
  13.2 1.1 convolution_convert_fusion.1
  14.3 1.1 convolution_convert_fusion
  15.4 1.9 pad_maximum_fusion.half_ref
  17.3 292.6 %shard_map.64 = (f32[2048,1024]{1,0:T(8,128)}, f32[2048,1024]{1,0:T(8,128)}, f32[16,128]{1,0:T(8,128)}, bf16[12,8,2,64,512]{4,3,2,1,0:T(8,128)(2,1)}) custom-call(bf16[2,12,2,64,512]{4,3,2,1,0:T(8,128)(2,1)} %pad_maximum_fusion.half_ref, bf16[512,512]{1,0:T(8,128)(2,1)} %constant.45.clone.table_ref), custom_call_target="tpu_custom_call" | custom-call | tf_op jit(solution)/shard_map/pallas_call | solution.py:388
  310.0 1.3 reduce_sum.9
  312.6 10.1 %select_add_fusion = f32[2048,1024]{1,0:T(8,128)} fusion(f32[2048,1024]{1,0:T(8,128)} %get-tuple-element.8, f32[2048,1024]{1,0:T(8,128)} %get-tuple-element.9, f32[]{:T(128)S(6)} %mul.37, s32[1024]{0:T(1024)S(1)} %iota_add_fusion.1, s32[2048]{0:T(1024)S(1)} %iota_add_fusion), kind=kLoop, calls=%fused_computation.1 | loop fusion | flops 10485760 | bytes 25178116 | tf_op jit(solution)/shard_map/add | solution.py:433
  (6 shorter events, 0.0 us)
Async XLA Ops:
  0.7 11.4 %copy-start = (s32[1536]{0:T(1024)S(1)}, s32[1536]{0:T(1024)}, u32[]{:S(2)}) copy-start(s32[1536]{0:T(1024)} %param.7) | copy-start | bytes 18436
  12.2 1.0 copy-start.1
  12.2 1.0 copy-start.2
where the time goes:
time: 325 us; the launch traced here: 323 us
  Pallas kernels  293 us (90%)
  other arithmetic  15 us (5%)
  local copies, waits for them, and re-layouts  11.5 us (4%)
    pallas_call x1, Pallas kernels, fused(): pl.pallas_call(functools.partial(fused_kernel, planes, chunks, rows, piec...  293 us
    gather x1, local copies, waits for them, and re-layouts, fused(): picked = jnp.take(row_bank, token_ids, axis=0)  11.4 us
    add x1, other arithmetic, damped(): return gram_block + damping[0] * mean_diag * on_diag  10.1 us

commit v1 on v0

--- a/solution.py
+++ b/solution.py
@@ -32,12 +32,12 @@
 
 
 def fused_kernel(
-    planes, chunks, rows, piece, scale,
+    planes, chunks, rows, piece, slots, scale,
     half_ref, table_ref,
-    gram_ref, gram_in_ref, square_ref, full_ref,
-    xbuf, tmp, rot, rxr, rxq, acc, squares,
+    gram_ref, square_ref, full_ref, hop_ref,
+    xbuf, tmp, rot, rxr, rxq, rxm, acc, squares,
     part_send, part_recv, z_send, z_recv, r_send, r_recv, q_send, q_recv,
-    s_send, s_recv, g_send, g_recv, load_sem, out_sem,
+    h_send, h_recv, m_send, m_recv, s_send, s_recv, load_sem, out_sem,
 ):
     tok = lax.axis_index("tok")
     col = lax.axis_index("col")
@@ -46,6 +46,7 @@
     ypos, xpos = tok // 2, tok % 2
     peers = {1: ypos * 2 + (1 - xpos), 2: (1 - ypos) * 2 + xpos, 3: 3 - tok}
     wide = 2 * piece
+    role = ((ypos + plane // 2) % 2) * 2 + (xpos + plane) % 2
 
     barrier = pltpu.get_barrier_semaphore()
     greet = [(tok, mate)]
@@ -90,57 +91,159 @@
             def _():
                 z_copy(k, mate, way).start()
 
+    def z_stage(k, distance):
+        for way, origin in ((0, plane - distance), (1, plane + distance)):
+            @pl.when((origin >= 0) & (origin < planes))
+            def _():
+                for side in (0, 1):
+                    j = origin * 2 + (core if side == 0 else 1 - core)
+                    z_copy(k, j, way).wait_recv()
+
+                    @pl.when(can[way])
+                    def _():
+                        z_copy(k, j, way).start()
+
+    def col_copy(k, m):
+        return pltpu.make_async_remote_copy(
+            src_ref=rot.at[k % slots, pl.ds(plane * wide, wide)],
+            dst_ref=rxq.at[k, :, pl.ds(m * rows, rows)],
+            send_sem=q_send.at[k, m], recv_sem=q_recv.at[k, m],
+            device_id=(peers[m], col), device_id_type=MESH)
+
+    def relay_copy(k, m):
+        return pltpu.make_async_remote_copy(
+            src_ref=rxq.at[k, :, pl.ds(m * rows, rows)],
+            dst_ref=rxq.at[k, :, pl.ds(3 * rows, rows)],
+            send_sem=q_send.at[k, 2 + m], recv_sem=q_recv.at[k, 3],
+            device_id=(peers[3 - m], col), device_id_type=MESH)
+
     def row_copy(k, m):
         return pltpu.make_async_remote_copy(
-            src_ref=rot.at[k, pl.ds(peers[m] * wide, wide)],
+            src_ref=rot.at[k % slots, pl.ds(peers[m] * wide, wide)],
             dst_ref=rxr.at[k, :, pl.ds(m * rows, rows)],
             send_sem=r_send.at[k, m], recv_sem=r_recv.at[k, m],
             device_id=(peers[m], col), device_id_type=MESH)
 
-    def col_copy(k, m):
-        return pltpu.make_async_remote_copy(
-            src_ref=rot.at[k, pl.ds(plane * wide, wide)],
-            dst_ref=rxq.at[k, :, pl.ds(m * rows, rows)],
-            send_sem=q_send.at[k, m], recv_sem=q_recv.at[k, m],
+    def hop_copy(k, m):
+        return pltpu.make_async_remote_copy(
+            src_ref=rot.at[k % slots, pl.ds(peers[3] * wide, wide)],
+            dst_ref=hop_ref.at[m - 1, k],
+            send_sem=r_send.at[k, 3], recv_sem=h_recv.at[k, m],
             device_id=(peers[m], col), device_id_type=MESH)
 
-    def relay_copy(k):
-        odd = k % 2
-        target = peers[2] * (1 - odd) + peers[1] * odd
-        start = pl.multiple_of((1 + odd) * rows, rows)
-        return pltpu.make_async_remote_copy(
-            src_ref=rxq.at[k, :, pl.ds(start, rows)],
-            dst_ref=rxq.at[k, :, pl.ds(3 * rows, rows)],
-            send_sem=q_send.at[k, 3], recv_sem=q_recv.at[k, 3],
-            device_id=(target, col), device_id_type=MESH)
-
-    def z_stage(k, distance):
-        for way, origin in ((0, plane - distance), (1, plane + distance)):
-            @pl.when((origin >= 0) & (origin < planes))
-            def _():
-                for side in (0, 1):
-                    j = origin * 2 + (core if side == 0 else 1 - core)
-                    z_copy(k, j, way).wait_recv()
-
-                    @pl.when(can[way])
-                    def _():
-                        z_copy(k, j, way).start()
-
-    def load_chunk(k):
+    def hop_forward(k, m):
+        return pltpu.make_async_remote_copy(
+            src_ref=hop_ref.at[m - 1, k],
+            dst_ref=rxr.at[k, :, pl.ds(3 * rows, rows)],
+            send_sem=h_send.at[k, m], recv_sem=r_recv.at[k, 3],
+            device_id=(peers[3 - m], col), device_id_type=MESH)
+
+    def turn(k):
+        return (k + 2 * core) % 4
+
+    def y_first(k, sender):
+        phase = turn(k)
+        return (
+            ((sender == 0) & (phase % 2 == 0))
+            | ((sender == 2) & (phase < 3))
+            | ((sender == 1) & (phase == 0))
+        )
+
+    def hops_here(k, m):
+        if m == 2:
+            return y_first(k, (role + 2) % 4)
+        sender = role + 1 - 2 * (role % 2)
+        return (sender != 3) & jnp.logical_not(y_first(k, sender))
+
+    def relays_here(k, m):
+        even = turn(k) % 2 == 0
+        if m == 1:
+            return (role >= 2) | ((role == 1) & even)
+        return (role == 3) | ((role == 2) & (turn(k) % 2 == 1))
+
+    def send_chunk(k):
+        for m in (1, 2):
+            col_copy(k, m).start()
+        hop = y_first(k, role)
+
+        @pl.when(hop)
+        def _():
+            hop_copy(k, 2).start()
+
+        @pl.when(jnp.logical_not(hop) & (role != 3))
+        def _():
+            hop_copy(k, 1).start()
+
+        for m in (1, 2):
+            @pl.when(role != m)
+            def _():
+                row_copy(k, m).start()
+
+    def sent_chunk(k):
+        for m in (1, 2):
+            col_copy(k, m).wait_send()
+        for m in (1, 2, 3):
+            @pl.when(role != m)
+            def _():
+                row_copy(k, m).wait_send()
+
+    def relay(k):
+        for m in (1, 2):
+            col_copy(k, m).wait_recv()
+
+            @pl.when(relays_here(k, m))
+            def _():
+                relay_copy(k, m).start()
+
+        for m in (1, 2):
+            @pl.when(hops_here(k, m))
+            def _():
+                hop_copy(k, m).wait_recv()
+                hop_forward(k, m).start()
+
+    def pass_rows(k, same):
+        source = rxq.at[k] if same else rxr.at[k, :, pl.ds(0, 4 * rows)]
+        return pltpu.make_async_remote_copy(
+            src_ref=source, dst_ref=rxr.at[k, :, pl.ds(4 * rows, 4 * rows)],
+            send_sem=m_send.at[k, 0], recv_sem=m_recv.at[k, 0],
+            device_id=(tok, mate), device_id_type=MESH)
+
+    def pass_cols(k):
+        return pltpu.make_async_remote_copy(
+            src_ref=rxq.at[k, pl.ds((1 - core) * piece, piece)], dst_ref=rxm.at[k],
+            send_sem=m_send.at[k, 1], recv_sem=m_recv.at[k, 1],
+            device_id=(tok, mate), device_id_type=MESH)
+
+    def arrivals(k):
+        relay_copy(k, 1).wait_recv()
+        pass_cols(k).start()
+
+        @pl.when(role != 0)
+        def _():
+            for m in (1, 2, 3):
+                row_copy(k, m).wait_recv()
+            pass_rows(k, False).start()
+
+        @pl.when(role == 0)
+        def _():
+            pass_rows(k, True).start()
+            for f in range(wide):
+                rxr[k, f, pl.ds(0, 4 * rows)] = rxq[k, f]
+
+    def loads(k):
         copies = [pltpu.make_async_copy(half_ref.at[core, k], xbuf.at[col], load_sem.at[0])]
         copies.append(pltpu.make_async_copy(full_ref.at[k, mate], xbuf.at[mate], load_sem.at[1]))
         for m in range(1, planes):
             other = ((plane + m) % planes) * 2
             copies.append(pltpu.make_async_copy(
                 full_ref.at[k, pl.ds(other, 2)], xbuf.at[pl.ds(other, 2)], load_sem.at[1 + m]))
-        for copy in copies:
-            copy.start()
-        for copy in copies:
-            copy.wait()
+        return copies
 
     groups = 2 * planes * piece
 
     def rotate(k):
+        slot = k % slots
+
         def product(j, carry):
             block = xbuf[j].reshape(piece * rows, LANES)
             out = jnp.dot(block, table_ref[...], preferred_element_type=jnp.float32)
@@ -163,7 +266,7 @@
             total = squares[0]
             for g in range(groups):
                 rounded = (values[g] * scale).astype(jnp.bfloat16)
-                rot[k, g, pl.ds(r, 16), pl.ds(lane, 128)] = rounded
+                rot[slot, g, pl.ds(r, 16), pl.ds(lane, 128)] = rounded
                 exact = rounded.astype(jnp.float32)
                 total = total + exact * exact
             squares[0] = total
@@ -171,65 +274,34 @@
 
         lax.fori_loop(0, (rows // 16) * (LANES // 128), butterfly, 0)
         for f in range(wide):
-            rxr[k, f, pl.ds(0, rows)] = rot[k, tok * wide + f]
-            rxq[k, f, pl.ds(0, rows)] = rot[k, plane * wide + f]
-        for m in (1, 2):
-            col_copy(k, m).start()
-        for m in (1, 2, 3):
-            row_copy(k, m).start()
-
-    def relay(k):
-        odd = k % 2
-
-        @pl.when(odd == 0)
-        def _():
-            col_copy(k, 1).wait_recv()
-
-        @pl.when(odd == 1)
-        def _():
-            col_copy(k, 2).wait_recv()
-
-        relay_copy(k).start()
-
-    def arrivals(k):
-        odd = k % 2
-
-        @pl.when(odd == 0)
-        def _():
-            col_copy(k, 2).wait_recv()
-
-        @pl.when(odd == 1)
-        def _():
-            col_copy(k, 1).wait_recv()
-
-        for m in (1, 2, 3):
-            row_copy(k, m).wait_recv()
-        relay_copy(k).wait_recv()
+            rxr[k, f, pl.ds(0, rows)] = rot[slot, tok * wide + f]
+            rxq[k, f, pl.ds(0, rows)] = rot[slot, plane * wide + f]
+        send_chunk(k)
 
     def row_block(k, f):
         left = rxr[k, f].T
         start = pl.multiple_of(f * LANES, LANES)
-        for n in range(wide):
-            out = jnp.dot(left, rxq[k, n], preferred_element_type=jnp.float32)
-            acc[n // piece, pl.ds(start, LANES), pl.ds((n % piece) * LANES, LANES)] += out
+        for n in range(piece):
+            right = jnp.concatenate([rxq[k, core * piece + n], rxm[k, n]], axis=0)
+            out = jnp.dot(left, right, preferred_element_type=jnp.float32)
+            acc[pl.ds(start, LANES), pl.ds(n * LANES, LANES)] += out
+
+    def joined(k):
+        pass_cols(k).wait_recv()
+        pass_rows(k, False).wait_recv()
 
     def gram(k):
+        joined(k)
+
         def body(f, carry):
             row_block(k, f)
             return carry
 
         lax.fori_loop(0, wide, body, 0)
 
-    def gram_out(f):
-        span = pl.ds(pl.multiple_of(f * LANES, LANES), LANES)
-        return pltpu.make_async_remote_copy(
-            src_ref=acc.at[1 - core, span], dst_ref=gram_in_ref.at[span],
-            send_sem=g_send.at[f], recv_sem=g_recv.at[f],
-            device_id=(tok, mate), device_id_type=MESH)
-
     def gram_keep(f):
         span = pl.ds(pl.multiple_of(f * LANES, LANES), LANES)
-        return pltpu.make_async_copy(acc.at[core, span], gram_ref.at[span], out_sem.at[f])
+        return pltpu.make_async_copy(acc.at[span], gram_ref.at[span], out_sem.at[f])
 
     def square_copy(m):
         target = (tok, mate) if m == 4 else (peers[m % 4], col if m < 4 else mate)
@@ -247,32 +319,39 @@
     squares[0] = jnp.zeros((16, 128), jnp.float32)
 
     def clear(index, carry):
-        start = pl.multiple_of((index % (acc.shape[1] // 64)) * 64, 64)
-        acc[index // (acc.shape[1] // 64), pl.ds(start, 64)] = jnp.zeros((64, acc.shape[2]), jnp.float32)
-        return carry
-
-    lax.fori_loop(0, acc.shape[0] * (acc.shape[1] // 64), clear, 0)
+        start = pl.multiple_of(index * 64, 64)
+        acc[pl.ds(start, 64)] = jnp.zeros((64, acc.shape[1]), jnp.float32)
+        return carry
+
+    lax.fori_loop(0, acc.shape[0] // 64, clear, 0)
     for distance in range(1, planes - 1):
         z_stage(0, distance)
-    if chunks > 1:
-        own_sends(1)
+    for k in range(1, LEAD):
+        own_sends(k)
 
     def step(k, carry):
         z_stage(k, planes - 1)
-        if planes > 2:
-            @pl.when(k + 1 < chunks)
-            def _():
-                z_stage(k + 1, 1)
-
-        @pl.when(k + 2 < chunks)
-        def _():
-            own_sends(k + 2)
-
-        @pl.when(k > 0)
-        def _():
-            relay(k - 1)
-
-        load_chunk(k)
+        for copy in loads(k):
+            copy.start()
+
+        @pl.when(k + 1 < chunks)
+        def _():
+            z_stage(k + 1, 1)
+
+        @pl.when(k + LEAD < chunks)
+        def _():
+            own_sends(k + LEAD)
+
+        @pl.when(k >= RELAY_LAG)
+        def _():
+            relay(k - RELAY_LAG)
+
+        @pl.when(k >= slots)
+        def _():
+            sent_chunk(k - slots)
+
+        for copy in loads(k):
+            copy.wait()
         rotate(k)
 
         @pl.when(k + 1 < chunks)
@@ -280,10 +359,13 @@
             for distance in range(2, planes - 1):
                 z_stage(k + 1, distance)
 
-        @pl.when(k > 1)
-        def _():
-            arrivals(k - 2)
-            gram(k - 2)
+        @pl.when(k >= LAG)
+        def _():
+            arrivals(k - LAG)
+
+        @pl.when(k > LAG)
+        def _():
+            gram(k - LAG - 1)
 
         return carry
 
@@ -291,31 +373,34 @@
     for m in range(1, 8):
         square_copy(m).start()
     last = chunks - 1
-    if chunks > 1:
-        arrivals(last - 1)
-        gram(last - 1)
-    relay(last)
-    arrivals(last)
+    for k in range(chunks - RELAY_LAG, chunks):
+        relay(k)
+
+    def tail(k, carry):
+        arrivals(k)
+        gram(k - 1)
+        return carry
+
+    lax.fori_loop(chunks - LAG, chunks, tail, 0)
+    joined(last)
 
     def final(f, carry):
         row_block(last, f)
 
         @pl.when(f > 0)
         def _():
-            gram_out(f - 1).start()
             gram_keep(f - 1).start()
 
         return carry
 
     lax.fori_loop(0, wide, final, 0)
+    gram_keep(wide - 1).start()
     for m in range(1, 8):
         square_copy(m).wait()
     sums = squares[0]
     for m in range(1, 8):
         sums = sums + squares[m]
-    square_ref[...] = sums
-    gram_out(wide - 1).start()
-    gram_keep(wide - 1).start()
+    square_ref[...] = jnp.full(square_ref.shape, jnp.sum(sums), jnp.float32)
 
     def drain(k, carry):
         part_copy(k).wait_send()
@@ -328,20 +413,37 @@
             def _():
                 z_copy(k, j, 1).wait_send()
         for m in (1, 2):
-            col_copy(k, m).wait_send()
-        relay_copy(k).wait_send()
-        for m in (1, 2, 3):
-            row_copy(k, m).wait_send()
+            @pl.when(relays_here(k, m))
+            def _():
+                relay_copy(k, m).wait_send()
+
+        for m in (1, 2):
+            @pl.when(hops_here(k, m))
+            def _():
+                hop_forward(k, m).wait_send()
+
+        @pl.when(k >= chunks - slots)
+        def _():
+            sent_chunk(k)
+
+        pass_rows(k, False).wait_send()
+        pass_cols(k).wait_send()
         return carry
 
     lax.fori_loop(0, chunks, drain, 0)
 
     def finish(f, carry):
-        gram_out(f).wait()
         gram_keep(f).wait()
         return carry
 
     lax.fori_loop(0, wide, finish, 0)
+
+
+ROWS = 32
+SLOTS = 6
+LEAD = 4
+RELAY_LAG = 2
+LAG = 4
 
 
 def fits(row_bank, token_ids):
@@ -350,10 +452,11 @@
     return (
         col_width % LANES == 0
         and tok_count == 4
-        and col_count % 2 == 0
+        and col_count == 8
         and D // tok_count == 2 * col_width
-        and tok_rows % 256 == 0
-        and tok_rows * D * 6 + (D // tok_count) ** 2 * 4 <= 96 * 2**20
+        and tok_rows % (2 * ROWS) == 0
+        and tok_rows // (2 * ROWS) >= SLOTS
+        and tok_rows * D * 7 // 2 + D // tok_count * col_width * 4 <= 54 * 2**20
     )
 
 
@@ -363,9 +466,8 @@
     tok_count = lax.axis_size("tok")
     tok_rows = token_ids.shape[0]
     planes = col_count // 2
-    own_rows = tok_rows // 2
-    rows = 64
-    chunks = own_rows // rows
+    rows = ROWS
+    chunks = tok_rows // 2 // rows
     piece = col_width // LANES
     wide = 2 * piece
     groups = D // LANES
@@ -373,7 +475,7 @@
     inner = jnp.asarray(np.kron(np.eye(spread), sylvester(BLOCK)), jnp.bfloat16)
     outer = jnp.asarray(np.kron(sylvester(spread), np.eye(BLOCK)), jnp.bfloat16)
     signs = sign_flips.astype(jnp.bfloat16)[:, None]
-    picked = jnp.take(row_bank, token_ids, axis=0)
+    picked = row_bank.at[token_ids].get(mode="promise_in_bounds")
     parts = []
     for g in range(piece):
         part = picked[:, g * LANES : (g + 1) * LANES]
@@ -385,30 +487,32 @@
     vmem = pl.BlockSpec(memory_space=pltpu.VMEM)
     dma = pltpu.SemaphoreType.DMA
     height = D // tok_count
-    gram, gram_in, squares, _ = pl.pallas_call(
-        functools.partial(fused_kernel, planes, chunks, rows, piece, 1.0 / math.sqrt(D)),
+    gram, squares, _, _ = pl.pallas_call(
+        functools.partial(fused_kernel, planes, chunks, rows, piece, SLOTS, 1.0 / math.sqrt(D)),
         out_shape=(
             jax.ShapeDtypeStruct((height, col_width), jnp.float32),
-            jax.ShapeDtypeStruct((height, col_width), jnp.float32),
-            jax.ShapeDtypeStruct((16, 128), jnp.float32),
+            jax.ShapeDtypeStruct((8, 128), jnp.float32),
             jax.ShapeDtypeStruct((chunks, col_count, piece, rows, LANES), jnp.bfloat16),
+            jax.ShapeDtypeStruct((2, chunks, wide, rows, LANES), jnp.bfloat16),
         ),
         in_specs=[any_space, vmem],
-        out_specs=(any_space, any_space, vmem, any_space),
+        out_specs=(any_space, vmem, any_space, any_space),
         scratch_shapes=[
             pltpu.VMEM((col_count, piece, rows, LANES), jnp.bfloat16),
             pltpu.VMEM((groups, rows, LANES), jnp.float32),
-            pltpu.VMEM((chunks, groups, rows, LANES), jnp.bfloat16),
+            pltpu.VMEM((SLOTS, groups, rows, LANES), jnp.bfloat16),
+            pltpu.VMEM((chunks, wide, 8 * rows, LANES), jnp.bfloat16),
             pltpu.VMEM((chunks, wide, 4 * rows, LANES), jnp.bfloat16),
-            pltpu.VMEM((chunks, wide, 4 * rows, LANES), jnp.bfloat16),
-            pltpu.VMEM((2, height, col_width), jnp.float32),
+            pltpu.VMEM((chunks, piece, 4 * rows, LANES), jnp.bfloat16),
+            pltpu.VMEM((height, col_width), jnp.float32),
             pltpu.VMEM((8, 16, 128), jnp.float32),
             dma((chunks,)), dma((chunks,)),
             dma((chunks, col_count, 2)), dma((chunks, col_count)),
             dma((chunks, 4)), dma((chunks, 4)),
-            dma((chunks, 4)), dma((chunks, 4)),
+            dma((chunks, 5)), dma((chunks, 4)),
+            dma((chunks, 3)), dma((chunks, 3)),
+            dma((chunks, 2)), dma((chunks, 2)),
             dma((8,)), dma((8,)),
-            dma((wide,)), dma((wide,)),
             dma((planes + 1,)), dma((wide,)),
         ],
         compiler_params=pltpu.CompilerParams(
@@ -416,9 +520,8 @@
         ),
     )(half, outer)
     tokens_all = tok_rows * tok_count
-    mean_diag = jnp.sum(squares) / tokens_all / D
-    gram_block = (gram + gram_in) / tokens_all
-    return damped(gram_block, damping, mean_diag)
+    mean_diag = squares[0, 0] / tokens_all / D
+    return damped(gram / tokens_all, damping, mean_diag)
 
 
 def damped(gram_block, damping, mean_diag):

time: 325 us -> 300 us (0.923)
  Pallas kernels: 293 us -> 273 us
  other arithmetic: 15 us -> 8.86 us
    pallas_call x1, Pallas kernels: 293 us -> 273 us  [fused(): pl.pallas_call(functools.partial(fused_kernel, planes, chunks, rows, piec...]
    add x1, other arithmetic: 10.1 us -> 6.19 us  [damped(): return gram_block + damping[0] * mean_diag * on_diag]
where the time goes in v1:
time: 300 us; the launch traced here: 299 us
  Pallas kernels  273 us (91%)
  local copies, waits for them, and re-layouts  12.6 us (4%)
  other arithmetic  8.86 us (3%)
  matrix products  3.23 us (1%)
    pallas_call x1, Pallas kernels, fused(): pl.pallas_call(functools.partial(fused_kernel, planes, chunks, rows, piec...  273 us
    gather x1, local copies, waits for them, and re-layouts, fused(): picked = row_bank.at[token_ids].get(mode='promise_in_bounds')  11.4 us
    add x1, other arithmetic, damped(): return gram_block + damping[0] * mean_diag * on_diag  6.19 us

profile of v1, /device:TPU:3, one launch (start us, length us, event | category | flops | bytes accessed | tf_op | source)
XLA Modules:
  0.0 299.4 jit_solution(16194538328388014782)
XLA Ops:
  0.0 0.7 compare_select_fusion
  0.7 0.0 copy-start
  0.7 11.4 %gather_fusion = bf16[1536,1024]{1,0:T(8,128)(2,1)S(1)} fusion(bf16[16384,1024]{1,0:T(8,128)(2,1)} %param.6, s32[2048]{0:T(1024)S(1)} %pad_clamp_fusion), kind=kCustom, calls=%fused_computation | custom fusion | bytes 6297600 | tf_op jit(solution)/shard_map/gather | solution.py:478
  12.1 0.0 copy-done
  12.2 0.0 copy-start.1
  12.2 2.2 convolution_convert_fusion.1
  14.4 0.0 copy-done.1
  14.4 1.1 convolution_convert_fusion
  15.4 1.9 pad_maximum_fusion.half_ref
  17.4 273.3 %shard_map.64 = (f32[2048,1024]{1,0:T(8,128)}, f32[8,128]{1,0:T(8,128)}, bf16[24,8,2,32,512]{4,3,2,1,0:T(8,128)(2,1)}, bf16[2,24,4,32,512]{4,3,2,1,0:T(8,128)(2,1)}) custom-call(bf16[2,24,2,32,512]{4,3,2,1,0:T(8,128)(2,1)} %pad_maximum_fusion.half_ref, bf16[512,512]{1,0:T(8,128)(2,1)} %constant.33.clone.table_ref), custom_call_target="tpu_custom_call" | custom-call | tf_op jit(solution)/shard_map/pallas_call | solution.py:490
  290.7 1.2 slice.21
  293.3 6.2 %select_add_fusion = f32[2048,1024]{1,0:T(8,128)} fusion(f32[2048,1024]{1,0:T(8,128)} %get-tuple-element.7, f32[]{:T(128)S(6)} %mul.37, s32[1024]{0:T(1024)S(1)} %iota_add_fusion.1, s32[2048]{0:T(1024)S(1)} %iota_add_fusion), kind=kLoop, calls=%fused_computation.1 | loop fusion | flops 8388608 | bytes 16789508 | tf_op jit(solution)/shard_map/add | solution.py:536
  (5 shorter events, 0.0 us)
Async XLA Ops:
  0.7 11.4 %copy-start = (s32[1024]{0:T(1024)S(1)}, s32[1024]{0:T(1024)}, u32[]{:S(2)}) copy-start(s32[1024]{0:T(1024)} %param.8) | copy-start | bytes 12292
  12.2 2.2 copy-start.1

commit v2 on v1

v2 whole, which is shorter than its diff:
```python
import functools
import math

import jax
import jax.numpy as jnp
import numpy as np
from jax import lax
from jax.experimental import pallas as pl
from jax.experimental.pallas import tpu as pltpu
from jax.sharding import PartitionSpec as P

D = 8192
BLOCK = 32
LANES = 512
MESH = pl.DeviceIdType.MESH


def hadamard(order):
    index_range = jnp.arange(order, dtype=jnp.int32)
    anded = jnp.bitwise_and(index_range[:, None], index_range[None, :])
    parity = jnp.zeros((order, order), jnp.int32)
    for bit_place in range(int(order).bit_length()):
        parity = parity + jnp.bitwise_and(jnp.right_shift(anded, bit_place), 1)
    return (1 - 2 * jnp.bitwise_and(parity, 1)).astype(jnp.bfloat16)


def sylvester(order):
    table = np.ones((1, 1))
    while table.shape[0] < order:
        table = np.block([[table, table], [table, -table]])
    return table


def fused_kernel(
    planes, chunks, rows, piece, slots, scale, tokens_all,
    picked_ref, sign_ref, damp_ref, inner_ref, table_ref,
    gram_ref, full_ref, hop_ref,
    pick, half, xbuf, tmp, rot, rxr, rxq, rxm, acc, squares,
    part_send, part_recv, z_send, z_recv, sent, col_recv, in_recv, relay_send,
    h_send, h_recv, m_send, m_recv, s_send, s_recv, pick_sem, load_sem, out_sem,
):
    tok = lax.axis_index("tok")
    col = lax.axis_index("col")
    plane, core = col // 2, col % 2
    mate = plane * 2 + (1 - core)
    ypos, xpos = tok // 2, tok % 2
    peers = {1: ypos * 2 + (1 - xpos), 2: (1 - ypos) * 2 + xpos, 3: 3 - tok}
    wide = 2 * piece
    role = ((ypos + plane // 2) % 2) * 2 + (xpos + plane) % 2

    barrier = pltpu.get_barrier_semaphore()
    greet = [(tok, mate)]
    for m in (1, 2, 3):
        greet.append((peers[m], col))
        greet.append((peers[m], mate))
    for m in range(1, planes):
        greet.append((tok, ((plane + m) % planes) * 2 + core))
    for device in greet:
        pl.semaphore_signal(barrier, inc=1, device_id=device, device_id_type=MESH)

    def pick_copies(k):
        slot = k % 2
        return [
            pltpu.make_async_copy(
                picked_ref.at[side, k], pick.at[slot, side], pick_sem.at[slot, side])
            for side in (0, 1)
        ]

    def fetch(k):
        for copy in pick_copies(k):
            copy.start()

    def turn_half(k):
        slot = k % 2
        for copy in pick_copies(k):
            copy.wait()
        signed = []
        for g in range(piece):
            lanes = pl.ds(g * LANES, LANES)
            signs = sign_ref[:, lanes].astype(jnp.float32).astype(jnp.bfloat16)
            for side in (0, 1):
                signed.append(pick[slot, side, :, lanes] * signs)
        out = jnp.dot(
            jnp.concatenate(signed, axis=0), inner_ref[...], preferred_element_type=jnp.float32
        ).astype(jnp.bfloat16)
        for g in range(piece):
            for side in (0, 1):
                start = (2 * g + side) * rows
                half[side, k, g] = out[start : start + rows]

    def part_copy(k):
        return pltpu.make_async_remote_copy(
            src_ref=half.at[1 - core, k], dst_ref=full_ref.at[k, col],
            send_sem=part_send.at[k % RING], recv_sem=part_recv.at[k],
            device_id=(tok, mate), device_id_type=MESH)

    def part_arrival(k):
        return pltpu.make_async_remote_copy(
            src_ref=half.at[1 - core, k], dst_ref=full_ref.at[k, mate],
            send_sem=part_send.at[k % RING], recv_sem=part_recv.at[k],
            device_id=(tok, mate), device_id_type=MESH)

    def z_copy(k, origin, way, source, target):
        own = (origin == plane) & (way == 1)
        return pltpu.make_async_remote_copy(
            src_ref=source, dst_ref=target,
            send_sem=z_send.at[k % RING, jnp.where(own, planes, origin)],
            recv_sem=z_recv.at[k, origin],
            device_id=(tok, col + 2 - 4 * way), device_id_type=MESH)

    def z_both(k, origin, way):
        both = full_ref.at[k, pl.ds(2 * origin, 2)]
        return z_copy(k, origin, way, both, both)

    can = {0: plane < planes - 1, 1: plane > 0}

    def own_sends(k):
        for way in (0, 1):
            @pl.when(can[way])
            def _():
                z_copy(k, plane, way, half.at[core, k], full_ref.at[k, col]).start()
        part_arrival(k).wait_recv()
        for way in (0, 1):
            @pl.when(can[way])
            def _():
                z_copy(k, plane, way, full_ref.at[k, mate], full_ref.at[k, mate]).start()

    def z_stage(k, distance):
        for way, origin in ((0, plane - distance), (1, plane + distance)):
            @pl.when((origin >= 0) & (origin < planes))
            def _():
                z_both(k, origin, way).wait_recv()

                @pl.when(can[way])
                def _():
                    z_both(k, origin, way).start()

    def place(k, m):
        return pl.ds(pl.multiple_of((k % 2) * 4 * rows + m * rows, rows), rows)

    def col_copy(k, m):
        return pltpu.make_async_remote_copy(
            src_ref=rot.at[k % slots, pl.ds(plane * wide, wide)],
            dst_ref=rxq.at[k // 2, :, place(k, m)],
            send_sem=sent.at[k % slots], recv_sem=col_recv.at[k],
            device_id=(peers[m], col), device_id_type=MESH)

    def relay_copy(k, m):
        return pltpu.make_async_remote_copy(
            src_ref=rxq.at[k // 2, :, place(k, m)],
            dst_ref=rxq.at[k // 2, :, place(k, 3)],
            send_sem=relay_send.at[k % RING, m - 1], recv_sem=in_recv.at[k // 2],
            device_id=(peers[3 - m], col), device_id_type=MESH)

    def row_copy(k, m):
        return pltpu.make_async_remote_copy(
            src_ref=rot.at[k % slots, pl.ds(peers[m] * wide, wide)],
            dst_ref=rxr.at[k // 2, :, place(k, m)],
            send_sem=sent.at[k % slots], recv_sem=in_recv.at[k // 2],
            device_id=(peers[m], col), device_id_type=MESH)

    def hop_copy(k, m):
        return pltpu.make_async_remote_copy(
            src_ref=rot.at[k % slots, pl.ds(peers[3] * wide, wide)],
            dst_ref=hop_ref.at[m - 1, k],
            send_sem=sent.at[k % slots], recv_sem=h_recv.at[k, m - 1],
            device_id=(peers[m], col), device_id_type=MESH)

    def hop_forward(k, m):
        return pltpu.make_async_remote_copy(
            src_ref=hop_ref.at[m - 1, k],
            dst_ref=rxr.at[k // 2, :, place(k, 3)],
            send_sem=h_send.at[k % RING, m - 1], recv_sem=in_recv.at[k // 2],
            device_id=(peers[3 - m], col), device_id_type=MESH)

    def turn(k):
        return (k + 2 * core) % 4

    def y_first(k, sender):
        phase = turn(k)
        return (
            ((sender == 0) & (phase % 2 == 0))
            | ((sender == 2) & (phase < 3))
            | ((sender == 1) & (phase == 0))
        )

    def hops_here(k, m):
        if m == 2:
            return y_first(k, (role + 2) % 4)
        sender = role + 1 - 2 * (role % 2)
        return (sender != 3) & jnp.logical_not(y_first(k, sender))

    def relays_here(k, m):
        even = turn(k) % 2 == 0
        if m == 1:
            return (role >= 2) | ((role == 1) & even)
        return (role == 3) | ((role == 2) & (turn(k) % 2 == 1))

    def send_chunk(k):
        for m in (1, 2):
            col_copy(k, m).start()
        hop = y_first(k, role)

        @pl.when(hop)
        def _():
            hop_copy(k, 2).start()

        @pl.when(jnp.logical_not(hop) & (role != 3))
        def _():
            hop_copy(k, 1).start()

        for m in (1, 2):
            @pl.when(role != m)
            def _():
                row_copy(k, m).start()

    def blocks(count, send_sem, recv_sem):
        area = hop_ref.at[0, pl.ds(0, count)]
        return pltpu.make_async_remote_copy(
            src_ref=area, dst_ref=area, send_sem=send_sem, recv_sem=recv_sem,
            device_id=(peers[1], col), device_id_type=MESH)

    def sent_chunk(k):
        slot = sent.at[k % slots]

        @pl.when(role == 0)
        def _():
            blocks(5, slot, col_recv.at[0]).wait_send()

        @pl.when(role != 0)
        def _():
            blocks(4, slot, col_recv.at[0]).wait_send()

    def relay(k):
        blocks(2, sent.at[0], col_recv.at[k]).wait_recv()
        for m in (1, 2):
            @pl.when(relays_here(k, m))
            def _():
                relay_copy(k, m).start()

        for m in (1, 2):
            @pl.when(hops_here(k, m))
            def _():
                hop_copy(k, m).wait_recv()
                hop_forward(k, m).start()

    def pass_rows(p, same):
        source = rxq.at[p] if same else rxr.at[p, :, pl.ds(0, 8 * rows)]
        return pltpu.make_async_remote_copy(
            src_ref=source, dst_ref=rxr.at[p, :, pl.ds(8 * rows, 8 * rows)],
            send_sem=m_send.at[p, 0], recv_sem=m_recv.at[p, 0],
            device_id=(tok, mate), device_id_type=MESH)

    def pass_cols(p):
        return pltpu.make_async_remote_copy(
            src_ref=rxq.at[p, pl.ds((1 - core) * piece, piece)], dst_ref=rxm.at[p],
            send_sem=m_send.at[p, 1], recv_sem=m_recv.at[p, 1],
            device_id=(tok, mate), device_id_type=MESH)

    def arrivals(p):
        @pl.when(role != 0)
        def _():
            blocks(8, sent.at[0], in_recv.at[p]).wait_recv()
            pass_rows(p, False).start()

        @pl.when(role == 0)
        def _():
            blocks(2, sent.at[0], in_recv.at[p]).wait_recv()
            pass_rows(p, True).start()
            for f in range(wide):
                rxr[p, f, pl.ds(0, 8 * rows)] = rxq[p, f]

        pass_cols(p).start()

    def loads(k):
        copies = [pltpu.make_async_copy(full_ref.at[k, mate], xbuf.at[mate], load_sem.at[1])]
        for m in range(1, planes):
            other = ((plane + m) % planes) * 2
            copies.append(pltpu.make_async_copy(
                full_ref.at[k, pl.ds(other, 2)], xbuf.at[pl.ds(other, 2)], load_sem.at[1 + m]))
        return copies

    groups = 2 * planes * piece

    def rotate(k):
        slot = k % slots

        block = xbuf[...].reshape(groups * rows, LANES)
        out = jnp.dot(block, table_ref[...], preferred_element_type=jnp.float32)
        tmp[...] = out.reshape(groups, rows, LANES)

        def butterfly(index, carry):
            r = pl.multiple_of((index // (LANES // 128)) * 16, 16)
            lane = pl.multiple_of((index % (LANES // 128)) * 128, 128)
            values = [tmp[g, pl.ds(r, 16), pl.ds(lane, 128)] for g in range(groups)]
            step = 1
            while step < groups:
                values = [
                    values[g] + values[g + step] if g & step == 0 else values[g - step] - values[g]
                    for g in range(groups)
                ]
                step *= 2
            total = squares[0]
            for g in range(groups):
                rounded = (values[g] * scale).astype(jnp.bfloat16)
                rot[slot, g, pl.ds(r, 16), pl.ds(lane, 128)] = rounded
                exact = rounded.astype(jnp.float32)
                total = total + exact * exact
            squares[0] = total
            return carry

        lax.fori_loop(0, (rows // 16) * (LANES // 128), butterfly, 0)
        for f in range(wide):
            rxr[k // 2, f, place(k, 0)] = rot[slot, tok * wide + f]
            rxq[k // 2, f, place(k, 0)] = rot[slot, plane * wide + f]
        send_chunk(k)

    def row_block(k, f):
        left = rxr[k, f].T
        start = pl.multiple_of(f * LANES, LANES)
        for n in range(piece):
            right = jnp.concatenate([rxq[k, core * piece + n], rxm[k, n]], axis=0)
            out = jnp.dot(left, right, preferred_element_type=jnp.float32)
            acc[pl.ds(start, LANES), pl.ds(n * LANES, LANES)] += out

    def joined(k):
        pass_cols(k).wait_recv()
        pass_rows(k, False).wait_recv()

    def gram(k):
        joined(k)

        def body(f, carry):
            row_block(k, f)
            return carry

        lax.fori_loop(0, wide, body, 0)

    def gram_keep(f):
        span = pl.ds(pl.multiple_of(f * LANES, LANES), LANES)
        return pltpu.make_async_copy(acc.at[span], gram_ref.at[span], out_sem.at[f])

    def square_copy(m):
        target = (tok, mate) if m == 4 else (peers[m % 4], col if m < 4 else mate)
        return pltpu.make_async_remote_copy(
            src_ref=squares.at[0], dst_ref=squares.at[m],
            send_sem=s_send.at[0], recv_sem=s_recv.at[0],
            device_id=target, device_id_type=MESH)

    def squares_done():
        return pltpu.make_async_remote_copy(
            src_ref=squares.at[pl.ds(1, 7)], dst_ref=squares.at[pl.ds(1, 7)],
            send_sem=s_send.at[0], recv_sem=s_recv.at[0],
            device_id=(tok, mate), device_id_type=MESH)

    fetch(0)
    fetch(1)
    turn_half(0)
    pl.semaphore_wait(barrier, len(greet))
    part_copy(0).start()
    own_sends(0)
    fetch(2)
    squares[0] = jnp.zeros((16, 128), jnp.float32)

    def clear(index, carry):
        start = pl.multiple_of(index * 64, 64)
        acc[pl.ds(start, 64)] = jnp.zeros((64, acc.shape[1]), jnp.float32)
        return carry

    lax.fori_loop(0, acc.shape[0] // 64, clear, 0)
    for distance in range(1, planes - 1):
        turn_half(distance)
        fetch(distance + 2)
        part_copy(distance).start()
        z_stage(0, distance)
        own_sends(distance)
    for k in range(planes - 1, LEAD + 1):
        turn_half(k)
        fetch(k + 2)
        part_copy(k).start()
    for k in range(planes - 1, LEAD):
        own_sends(k)

    def drain(k):
        part_copy(k).wait_send()
        for origin in range(planes):
            @pl.when(can[0] & (origin <= plane))
            def _():
                z_both(k, origin, 0).wait_send()

            @pl.when(can[1] & (origin >= plane))
            def _():
                z_both(k, origin, 1).wait_send()
        for m in (1, 2):
            @pl.when(relays_here(k, m))
            def _():
                relay_copy(k, m).wait_send()

            @pl.when(hops_here(k, m))
            def _():
                hop_forward(k, m).wait_send()

    def step(k, carry):
        z_stage(k, planes - 1)
        for copy in loads(k):
            copy.start()

        @pl.when(k + 1 < chunks)
        def _():
            z_stage(k + 1, 1)

        @pl.when(k + LEAD < chunks)
        def _():
            own_sends(k + LEAD)

        @pl.when(k + LEAD + 1 < chunks)
        def _():
            turn_half(k + LEAD + 1)
            part_copy(k + LEAD + 1).start()

        @pl.when(k + LEAD + 3 < chunks)
        def _():
            fetch(k + LEAD + 3)

        @pl.when(k >= RELAY_LAG)
        def _():
            relay(k - RELAY_LAG)

        @pl.when(k >= slots)
        def _():
            sent_chunk(k - slots)

        for copy in loads(k):
            copy.wait()
        xbuf[col] = half[core, k]
        rotate(k)

        @pl.when(k + 1 < chunks)
        def _():
            for distance in range(2, planes - 1):
                z_stage(k + 1, distance)

        @pl.when((k % 2 == 1) & (k // 2 >= LAG))
        def _():
            arrivals(k // 2 - LAG)

        @pl.when((k % 2 == 1) & (k // 2 > LAG))
        def _():
            gram(k // 2 - LAG - 1)

        @pl.when(k >= DRAIN)
        def _():
            drain(k - DRAIN)

        return carry

    lax.fori_loop(0, chunks, step, 0)
    for m in range(1, 8):
        square_copy(m).start()
    pairs = chunks // 2
    last = pairs - 1
    for k in range(chunks - RELAY_LAG, chunks):
        relay(k)

    def tail(p, carry):
        arrivals(p)
        gram(p - 1)
        for k in (0, 1):
            drain(2 * (p + LAG) - DRAIN + k)
        return carry

    lax.fori_loop(pairs - LAG, pairs, tail, 0)
    squares_done().wait()
    sums = squares[0]
    for m in range(1, 8):
        sums = sums + squares[m]
    lift = damp_ref[0] * (jnp.sum(sums) / D)
    joined(last)

    def final(f, carry):
        left = rxr[last, f].T
        start = pl.multiple_of(f * LANES, LANES)
        for n in range(piece):
            right = jnp.concatenate([rxq[last, core * piece + n], rxm[last, n]], axis=0)
            out = jnp.dot(left, right, preferred_element_type=jnp.float32)
            here = (pl.ds(start, LANES), pl.ds(n * LANES, LANES))
            acc[here] += out

            @pl.when((role == 0) & (f == core * piece + n))
            def _():
                row = lax.broadcasted_iota(jnp.int32, (LANES, LANES), 0)
                column = lax.broadcasted_iota(jnp.int32, (LANES, LANES), 1)
                acc[here] += lift * (row == column).astype(jnp.float32)

        @pl.when(f > 0)
        def _():
            gram_keep(f - 1).start()

        return carry

    lax.fori_loop(0, wide, final, 0)
    gram_keep(wide - 1).start()

    def rest(k, carry):
        @pl.when(k < pairs)
        def _():
            pass_rows(k, False).wait_send()
            pass_cols(k).wait_send()

        @pl.when(k >= chunks - DRAIN + 2 * LAG)
        def _():
            drain(k)

        @pl.when(k >= chunks - slots)
        def _():
            sent_chunk(k)

        return carry

    lax.fori_loop(0, chunks, rest, 0)

    def finish(f, carry):
        gram_keep(f).wait()
        return carry

    lax.fori_loop(0, wide, finish, 0)


ROWS = 16
SLOTS = 12
LEAD = 6
RELAY_LAG = 3
LAG = 3
DRAIN = 12
RING = 20


def fits(row_bank, token_ids):
    col_width, tok_rows = row_bank.shape[1], token_ids.shape[0]
    col_count, tok_count = lax.axis_size("col"), lax.axis_size("tok")
    return (
        col_width % LANES == 0
        and tok_count == 4
        and col_count == 8
        and D // tok_count == 2 * col_width
        and tok_rows % (4 * ROWS) == 0
        and tok_rows // (2 * ROWS) >= DRAIN
        and tok_rows * D * 7 // 2 + D // tok_count * col_width * 4 <= 54 * 2**20
    )


def fused(row_bank, token_ids, sign_flips, damping):
    col_width = row_bank.shape[1]
    col_count = lax.axis_size("col")
    tok_count = lax.axis_size("tok")
    tok_rows = token_ids.shape[0]
    planes = col_count // 2
    rows = ROWS
    chunks = tok_rows // 2 // rows
    piece = col_width // LANES
    wide = 2 * piece
    groups = D // LANES
    spread = LANES // BLOCK
    inner = jnp.asarray(np.kron(np.eye(spread), sylvester(BLOCK)), jnp.bfloat16)
    outer = jnp.asarray(np.kron(sylvester(spread), np.eye(BLOCK)), jnp.bfloat16)
    picked = row_bank.at[token_ids].get(
        mode="promise_in_bounds", wrap_negative_indices=False
    ).reshape(2, chunks, rows, col_width)
    any_space = pl.BlockSpec(memory_space=pl.ANY)
    vmem = pl.BlockSpec(memory_space=pltpu.VMEM)
    dma = pltpu.SemaphoreType.DMA
    height = D // tok_count
    gram, _, _ = pl.pallas_call(
        functools.partial(fused_kernel, planes, chunks, rows, piece, SLOTS, 1.0 / math.sqrt(D),
                          tok_rows * tok_count),
        out_shape=(
            jax.ShapeDtypeStruct((height, col_width), jnp.float32),
            jax.ShapeDtypeStruct((chunks, col_count, piece, rows, LANES), jnp.bfloat16),
            jax.ShapeDtypeStruct((2, chunks, wide, rows, LANES), jnp.bfloat16),
        ),
        in_specs=[any_space, vmem, pl.BlockSpec(memory_space=pltpu.SMEM), vmem, vmem],
        out_specs=(any_space, any_space, any_space),
        scratch_shapes=[
            pltpu.VMEM((2, 2, rows, col_width), jnp.bfloat16),
            pltpu.VMEM((2, chunks, piece, rows, LANES), jnp.bfloat16),
            pltpu.VMEM((col_count, piece, rows, LANES), jnp.bfloat16),
            pltpu.VMEM((groups, rows, LANES), jnp.float32),
            pltpu.VMEM((SLOTS, groups, rows, LANES), jnp.bfloat16),
            pltpu.VMEM((chunks // 2, wide, 16 * rows, LANES), jnp.bfloat16),
            pltpu.VMEM((chunks // 2, wide, 8 * rows, LANES), jnp.bfloat16),
            pltpu.VMEM((chunks // 2, piece, 8 * rows, LANES), jnp.bfloat16),
            pltpu.VMEM((height, col_width), jnp.float32),
            pltpu.VMEM((8, 16, 128), jnp.float32),
            dma((RING,)), dma((chunks,)),
            dma((RING, planes + 1)), dma((chunks, planes)),
            dma((SLOTS,)), dma((chunks,)), dma((chunks // 2,)), dma((RING, 2)),
            dma((RING, 2)), dma((chunks, 2)),
            dma((chunks // 2, 2)), dma((chunks // 2, 2)),
            dma((1,)), dma((1,)),
            dma((2, 2)), dma((planes + 1,)), dma((wide,)),
        ],
        compiler_params=pltpu.CompilerParams(
            collective_id=0, has_side_effects=True, vmem_limit_bytes=67043328
        ),
    )(picked, sign_flips[None, :], damping, inner, outer)
    return gram * jnp.float32(1.0 / (tok_rows * tok_count))


def damped(gram_block, damping, mean_diag):
    block_rows, col_width = gram_block.shape
    row_index = lax.axis_index("tok") * block_rows + lax.broadcasted_iota(
        jnp.int32, gram_block.shape, 0
    )
    col_index = lax.axis_index("col") * col_width + lax.broadcasted_iota(
        jnp.int32, gram_block.shape, 1
    )
    on_diag = (row_index == col_index).astype(jnp.float32)
    return gram_block + damping[0] * mean_diag * on_diag


def plain(row_bank, token_ids, sign_flips, damping):
    col_width = row_bank.shape[1]
    col_count = lax.axis_size("col")
    tok_count = lax.axis_size("tok")
    tok_rows = token_ids.shape[0]
    groups = D // BLOCK
    scale = 1.0 / math.sqrt(D)
    inner_table = hadamard(BLOCK)
    outer_table = hadamard(groups)
    col_start = lax.axis_index("col") * col_width
    picked = jnp.take(row_bank, token_ids, axis=0) * sign_flips.astype(jnp.bfloat16)[None, :]
    shaped = picked.reshape(picked.shape[0], -1, BLOCK)
    turned = jnp.einsum("rab,bc->rac", shaped, inner_table, preferred_element_type=jnp.float32)
    half_turned = turned.astype(jnp.bfloat16).reshape(picked.shape)
    grouped = half_turned.reshape(col_count, tok_rows // col_count, col_width)
    block = lax.all_to_all(grouped, "col", split_axis=0, concat_axis=2, tiled=True)[0]
    shaped = block.reshape(block.shape[0], groups, BLOCK)
    turned = (
        jnp.einsum("rab,ac->rcb", shaped, outer_table, preferred_element_type=jnp.float32) * scale
    )
    finished = turned.astype(jnp.bfloat16).reshape(block.shape)[None]
    squares = jnp.sum(jnp.square(finished.astype(jnp.float32)))
    tokens_all = tok_rows * tok_count
    square_sum = lax.psum(squares, ("tok", "col"))
    mean_diag = square_sum / tokens_all / D
    flat = lax.all_gather(finished, "col", axis=1, tiled=True).reshape(-1, D)
    own_cols = lax.dynamic_slice_in_dim(flat, col_start, col_width, 1)
    partial_sum = lax.dot_general(
        flat, own_cols, (((0,), (0,)), ((), ())), preferred_element_type=jnp.float32
    )
    gram_block = lax.psum_scatter(partial_sum, "tok", scatter_dimension=0, tiled=True) / tokens_all
    return damped(gram_block, damping, mean_diag)


def shards(row_bank, token_ids, sign_flips, damping):
    run = fused if fits(row_bank, token_ids) else plain
    return run(row_bank, token_ids, sign_flips, damping)


def solution(mesh):
    in_specs = (P(None, "col"), P("tok"), P("col"), P())
    out_specs = P("tok", "col")
    return jax.shard_map(shards, mesh=mesh, in_specs=in_specs, out_specs=out_specs, check_vma=False)
```

time: 300 us -> 289 us (0.963)
  Pallas kernels: 273 us -> 263 us
  matrix products: 3.23 us -> 0 us
    pallas_call x1, Pallas kernels: 273 us -> 263 us  [fused(): pl.pallas_call(functools.partial(fused_kernel, planes, chunks, rows, piec...]
    mul x0 -> x1, other arithmetic: none -> 8.78 us  [fused(): return gram * jnp.float32(1.0 / (tok_rows * tok_count))]
    add x3 -> x0, other arithmetic: 6.2 us -> none  [the longest x1 6.19 us: damped(): return gram_block + damping[0] * mean_diag * on_diag]
    dot_general x2 -> x0, matrix products: 3.23 us -> none  [fused(): jnp.dot(part, table, preferred_element_type=jnp.float32)]
where the time goes in v2:
time: 289 us; the launch traced here: 285 us
  Pallas kernels  263 us (91%)
  local copies, waits for them, and re-layouts  12.2 us (4%)
  other arithmetic  9.48 us (3%)
    pallas_call x1, Pallas kernels, fused(): pl.pallas_call(functools.partial(fused_kernel, planes, chunks, rows, piec...  263 us
    gather x1, local copies, waits for them, and re-layouts, fused(): row_bank.at[token_ids]  12.2 us
    mul x1, other arithmetic, fused(): return gram * jnp.float32(1.0 / (tok_rows * tok_count))  8.78 us

profile of v2, /device:TPU:3, one launch (start us, length us, event | category | flops | bytes accessed | tf_op | source)
XLA Modules:
  0.0 285.5 jit_solution(13150464927707368703)
XLA Ops:
  0.7 0.7 pad_clamp_fusion
  1.4 12.2 %gather_fusion = bf16[1536,1024]{1,0:T(8,128)(2,1)} fusion(bf16[16384,1024]{1,0:T(8,128)(2,1)} %param.6, s32[2048]{0:T(1024)S(1)} %pad_clamp_fusion), kind=kCustom, calls=%fused_computation | custom fusion | bytes 6297600 | tf_op jit(solution)/shard_map/gather | solution.py:566
  13.5 263.2 %shard_map.64 = (f32[2048,1024]{1,0:T(8,128)}, bf16[48,8,2,16,512]{4,3,2,1,0:T(8,128)(2,1)}, bf16[2,48,4,16,512]{4,3,2,1,0:T(8,128)(2,1)}) custom-call(bf16[2,48,16,1024]{3,2,1,0:T(8,128)(2,1)} %bitcast.2, s32[1,1024]{1,0:T(1,128)} %bitcast.3, f32[1]{0:T(128)S(6)} %copy.7.damp_ref, bf16[512,512]{1,0:T(8,128)(2,1)} %constant.6.clone.inner_ref, ...), custom_call_target="tpu_custom_call" | custom-call | tf_op jit(solution)/shard_map/pallas_call | solution.py:573
  276.7 8.8 %broadcast_multiply_fusion = f32[2048,1024]{1,0:T(8,128)} fusion(f32[2048,1024]{1,0:T(8,128)} %get-tuple-element.6), kind=kLoop, calls=%fused_computation.1 | loop fusion | flops 2097152 | bytes 16777216 | tf_op jit(solution)/shard_map/mul | solution.py:606

commit v3 on v2

--- a/solution.py
+++ b/solution.py
@@ -101,11 +101,10 @@
             device_id=(tok, mate), device_id_type=MESH)
 
     def z_copy(k, origin, way, source, target):
-        own = (origin == plane) & (way == 1)
         return pltpu.make_async_remote_copy(
             src_ref=source, dst_ref=target,
-            send_sem=z_send.at[k % RING, jnp.where(own, planes, origin)],
-            recv_sem=z_recv.at[k, origin],
+            send_sem=z_send.at[k % RING, origin + way],
+            recv_sem=z_recv.at[k, origin - way],
             device_id=(tok, col + 2 - 4 * way), device_id_type=MESH)
 
     def z_both(k, origin, way):
@@ -163,7 +162,7 @@
         return pltpu.make_async_remote_copy(
             src_ref=rot.at[k % slots, pl.ds(peers[3] * wide, wide)],
             dst_ref=hop_ref.at[m - 1, k],
-            send_sem=sent.at[k % slots], recv_sem=h_recv.at[k, m - 1],
+            send_sem=sent.at[k % slots], recv_sem=h_recv.at[k],
             device_id=(peers[m], col), device_id_type=MESH)
 
     def hop_forward(k, m):
@@ -238,26 +237,42 @@
             def _():
                 relay_copy(k, m).start()
 
-        for m in (1, 2):
-            @pl.when(hops_here(k, m))
-            def _():
-                hop_copy(k, m).wait_recv()
+        first, second = hops_here(k, 1), hops_here(k, 2)
+
+        @pl.when(first & second)
+        def _():
+            blocks(2, sent.at[0], h_recv.at[k]).wait_recv()
+
+        @pl.when(first != second)
+        def _():
+            blocks(1, sent.at[0], h_recv.at[k]).wait_recv()
+
+        for m, here in ((1, first), (2, second)):
+            @pl.when(here)
+            def _():
                 hop_forward(k, m).start()
 
     def pass_rows(p, same):
         source = rxq.at[p] if same else rxr.at[p, :, pl.ds(0, 8 * rows)]
         return pltpu.make_async_remote_copy(
             src_ref=source, dst_ref=rxr.at[p, :, pl.ds(8 * rows, 8 * rows)],
-            send_sem=m_send.at[p, 0], recv_sem=m_recv.at[p, 0],
+            send_sem=m_send.at[p % PASSES], recv_sem=m_recv.at[p],
             device_id=(tok, mate), device_id_type=MESH)
 
     def pass_cols(p):
         return pltpu.make_async_remote_copy(
             src_ref=rxq.at[p, pl.ds((1 - core) * piece, piece)], dst_ref=rxm.at[p],
-            send_sem=m_send.at[p, 1], recv_sem=m_recv.at[p, 1],
+            send_sem=m_send.at[p % PASSES], recv_sem=m_recv.at[p],
             device_id=(tok, mate), device_id_type=MESH)
 
+    def passed(p):
+        return blocks(12, m_send.at[p % PASSES], m_recv.at[p])
+
     def arrivals(p):
+        @pl.when(p >= PASSES)
+        def _():
+            passed(p - PASSES).wait_send()
+
         @pl.when(role != 0)
         def _():
             blocks(8, sent.at[0], in_recv.at[p]).wait_recv()
@@ -324,8 +339,7 @@
             acc[pl.ds(start, LANES), pl.ds(n * LANES, LANES)] += out
 
     def joined(k):
-        pass_cols(k).wait_recv()
-        pass_rows(k, False).wait_recv()
+        passed(k).wait_recv()
 
     def gram(k):
         joined(k)
@@ -502,11 +516,6 @@
     gram_keep(wide - 1).start()
 
     def rest(k, carry):
-        @pl.when(k < pairs)
-        def _():
-            pass_rows(k, False).wait_send()
-            pass_cols(k).wait_send()
-
         @pl.when(k >= chunks - DRAIN + 2 * LAG)
         def _():
             drain(k)
@@ -517,7 +526,9 @@
 
         return carry
 
-    lax.fori_loop(0, chunks, rest, 0)
+    lax.fori_loop(chunks - max(DRAIN, slots), chunks, rest, 0)
+    for p in range(pairs - PASSES, pairs):
+        passed(p).wait_send()
 
     def finish(f, carry):
         gram_keep(f).wait()
@@ -528,11 +539,12 @@
 
 ROWS = 16
 SLOTS = 12
-LEAD = 6
-RELAY_LAG = 3
+LEAD = 4
+RELAY_LAG = 2
 LAG = 3
-DRAIN = 12
-RING = 20
+DRAIN = 8
+RING = 14
+PASSES = 4
 
 
 def fits(row_bank, token_ids):
@@ -544,7 +556,7 @@
         and col_count == 8
         and D // tok_count == 2 * col_width
         and tok_rows % (4 * ROWS) == 0
-        and tok_rows // (2 * ROWS) >= DRAIN
+        and tok_rows // (2 * ROWS) >= 2 * SLOTS
         and tok_rows * D * 7 // 2 + D // tok_count * col_width * 4 <= 54 * 2**20
     )
 
@@ -592,10 +604,10 @@
             pltpu.VMEM((height, col_width), jnp.float32),
             pltpu.VMEM((8, 16, 128), jnp.float32),
             dma((RING,)), dma((chunks,)),
-            dma((RING, planes + 1)), dma((chunks, planes)),
+            dma((RING, planes + 1)), dma((chunks, planes - 1)),
             dma((SLOTS,)), dma((chunks,)), dma((chunks // 2,)), dma((RING, 2)),
-            dma((RING, 2)), dma((chunks, 2)),
-            dma((chunks // 2, 2)), dma((chunks // 2, 2)),
+            dma((RING, 2)), dma((chunks,)),
+            dma((PASSES,)), dma((chunks // 2,)),
             dma((1,)), dma((1,)),
             dma((2, 2)), dma((planes + 1,)), dma((wide,)),
         ],

time: 289 us -> 281 us (0.972)
  Pallas kernels: 263 us -> 256 us
    pallas_call x1, Pallas kernels: 263 us -> 256 us  [fused(): pl.pallas_call(functools.partial(fused_kernel, planes, chunks, rows, piec...]
where the time goes in v3:
time: 281 us; the launch traced here: 278 us
  Pallas kernels  256 us (91%)
  local copies, waits for them, and re-layouts  12.2 us (4%)
  other arithmetic  9.48 us (3%)
    pallas_call x1, Pallas kernels, fused(): pl.pallas_call(functools.partial(fused_kernel, planes, chunks, rows, piec...  256 us
    gather x1, local copies, waits for them, and re-layouts, fused(): row_bank.at[token_ids]  12.2 us
    mul x1, other arithmetic, fused(): return gram * jnp.float32(1.0 / (tok_rows * tok_count))  8.78 us

profile of v3, /device:TPU:3, one launch (start us, length us, event | category | flops | bytes accessed | tf_op | source)
XLA Modules:
  0.0 278.0 jit_solution(17080541935276419529)
XLA Ops:
  0.7 0.7 pad_clamp_fusion
  1.4 12.2 %gather_fusion = bf16[1536,1024]{1,0:T(8,128)(2,1)} fusion(bf16[16384,1024]{1,0:T(8,128)(2,1)} %param.6, s32[2048]{0:T(1024)S(1)} %pad_clamp_fusion), kind=kCustom, calls=%fused_computation | custom fusion | bytes 6297600 | tf_op jit(solution)/shard_map/gather | solution.py:578
  13.5 255.7 %shard_map.64 = (f32[2048,1024]{1,0:T(8,128)}, bf16[48,8,2,16,512]{4,3,2,1,0:T(8,128)(2,1)}, bf16[2,48,4,16,512]{4,3,2,1,0:T(8,128)(2,1)}) custom-call(bf16[2,48,16,1024]{3,2,1,0:T(8,128)(2,1)} %bitcast.2, s32[1,1024]{1,0:T(1,128)} %bitcast.3, f32[1]{0:T(128)S(6)} %copy.7.damp_ref, bf16[512,512]{1,0:T(8,128)(2,1)} %constant.6.clone.inner_ref, ...), custom_call_target="tpu_custom_call" | custom-call | tf_op jit(solution)/shard_map/pallas_call | solution.py:585
  269.3 8.8 %broadcast_multiply_fusion = f32[2048,1024]{1,0:T(8,128)} fusion(f32[2048,1024]{1,0:T(8,128)} %get-tuple-element.6), kind=kLoop, calls=%fused_computation.1 | loop fusion | flops 2097152 | bytes 16777216 | tf_op jit(solution)/shard_map/mul | solution.py:618
